TPU v7x, 32 devices: a whole 2x2x4 slice. The times are simulated.
32 devices in a mesh: grp: 4 (over y, core), mat: 8 (over z, x).
Axes of the slice: x: 2, y: 2, z: 4, core: 2. Of those that a mesh axis runs over, the one named last changes fastest.
Arguments:
- basis_values: bfloat16 [512, 256, 512], P(('grp', 'mat')), may hold values from -6 to 6
- weights: float32 [512, 256], P(('grp', 'mat')), may hold values from 0.004 to 0.04
- density: bfloat16 [192, 5, 128, 128], P('mat'), may hold values from -0.01171875 to 0.01171875
- block_live: int32 [192, 5], P('mat'), may hold values 0 or 1
- batch_blocks: int32 [512, 4], P(('grp', 'mat')), may hold values from 0 to 191, as said below
- live_functions: int32 [512], P(('grp', 'mat')), may hold values from 385 to 512
Outputs:
- site_density: float32 [512, 256], P(('grp', 'mat'))
- hamiltonian: bfloat16 [192, 5, 128, 128], P('mat', None, 'grp')
Inputs may be any that keep to these rules, and one draw needn't show every extreme that they name: `batch_blocks`: each row holds 4 increasing blocks within 5 consecutive blocks. The batches of device d are rows d * 16 to d * 16 + 15, counting devices grp first, and all their blocks lie in 8 consecutive block rows, the first of which is used by some batch of the device and the last by another; some batch spans 5 blocks.
All inputs are finite; a program needn't handle non-finite values. No bound on the sum of `block_live` on one device may be relied on, other than what follows from the above.
Results may differ from a plain program's by a relative error of at most 0.0049.
Values may be sent and summed in bfloat16 or wider, within the bound.
No kernel may reach another device: no remote copies, remote signals or barrier semaphores. Data moves between devices by JAX's collectives and lax.ppermute only.
A program may use at most 128 MiB of HBM per device.

v0:
```python
import jax
import jax.numpy as jnp
from jax import lax
from jax.sharding import PartitionSpec as P


def per_device(basis_values, weights, density, block_live, batch_blocks, live_functions):
    mat_count = lax.axis_size("mat")
    holder = lax.axis_index("mat")
    block_size = density.shape[-1]
    band_size = density.shape[1]
    slot_count = batch_blocks.shape[1]
    batch_width = slot_count * block_size
    local_rows = density.shape[0]
    point_count = weights.shape[1]
    region_first = jnp.min(batch_blocks)
    own_start = region_first.reshape(1)
    firsts = lax.all_gather(own_start, "mat", axis=0, tiled=True)
    wanted = firsts + (holder - firsts) % mat_count
    wanted_local = (wanted - holder) // mat_count
    live_mask = block_live.astype(jnp.bfloat16)
    outgoing = (
        jnp.take(density, wanted_local, axis=0)
        * jnp.take(live_mask, wanted_local, axis=0)[:, :, None, None]
    )
    incoming = lax.all_to_all(outgoing, "mat", split_axis=0, concat_axis=0, tiled=True)
    region = jnp.take(incoming, (region_first + jnp.arange(mat_count)) % mat_count, axis=0)
    function_index = jnp.arange(batch_width)
    slot_index = jnp.arange(slot_count)
    upper_half = slot_index[:, None] <= slot_index[None, :]
    steps_count = basis_values.shape[0] // 4
    step_inputs = (
        basis_values.reshape(steps_count, 4, point_count, batch_width),
        weights.reshape(steps_count, 4, point_count),
        batch_blocks.reshape(steps_count, 4, slot_count),
        live_functions.reshape(steps_count, 4),
    )

    def integrate(ham_region, inputs):
        values, point_weights, blocks, live_count = inputs
        values = jnp.where(
            function_index[None, None, :] < live_count[:, None, None],
            values,
            jnp.zeros_like(values),
        )
        lower_block = jnp.minimum(blocks[:, :, None], blocks[:, None, :])
        upper_block = jnp.maximum(blocks[:, :, None], blocks[:, None, :])
        row_index = lower_block - region_first
        offset = upper_block - lower_block
        gathered_tiles = region[row_index, offset]
        gathered_tiles = jnp.where(
            upper_half[None, :, :, None, None], gathered_tiles, jnp.swapaxes(gathered_tiles, -1, -2)
        )
        batch_matrix = gathered_tiles.transpose(0, 1, 3, 2, 4).reshape(4, batch_width, batch_width)
        product_rows = jnp.einsum(
            "brf,bfg->brg", values, batch_matrix, preferred_element_type=jnp.float32
        )
        site_values = jnp.sum(product_rows * values.astype(jnp.float32), axis=-1)
        potential = point_weights * site_values / jnp.sqrt(1.0 + site_values * site_values)
        weighted = (potential[:, :, None] * values.astype(jnp.float32)).astype(jnp.bfloat16)
        ham_batch = jnp.einsum("brf,brg->bfg", values, weighted, preferred_element_type=jnp.float32)
        ham_tiles = ham_batch.reshape(4, slot_count, block_size, slot_count, block_size).transpose(
            0, 1, 3, 2, 4
        )
        increment = jnp.where(
            upper_half[None, :, :, None, None], ham_tiles, jnp.zeros_like(ham_tiles)
        )
        ham_region = ham_region.at[row_index, offset].add(increment)
        return (ham_region, site_values)

    ham_region, site_values = lax.scan(
        integrate,
        jnp.zeros((mat_count, band_size, block_size, block_size), jnp.float32),
        step_inputs,
    )
    site_density = site_values.reshape(basis_values.shape[0], point_count)
    send_back = jnp.take(ham_region, (jnp.arange(mat_count) - region_first) % mat_count, axis=0)
    live_wide = block_live.astype(jnp.float32)[:, :, None, None]
    all_firsts = lax.all_gather(own_start, ("grp", "mat"), axis=0, tiled=True)
    groups_count = lax.axis_size("grp")
    pieces = send_back.reshape(
        mat_count, band_size, groups_count, block_size // groups_count, block_size
    )
    arrived = lax.all_to_all(
        lax.all_to_all(pieces, "grp", split_axis=2, concat_axis=2, tiled=True),
        "mat",
        split_axis=0,
        concat_axis=0,
        tiled=True,
    )
    firsts_grid = all_firsts.reshape(groups_count, mat_count)
    rows_grid = (firsts_grid + (holder - firsts_grid) % mat_count - holder) // mat_count
    selector = (rows_grid[None, :, :] == jnp.arange(local_rows)[:, None, None]).astype(jnp.float32)
    totals = (
        jnp.einsum("tgr,rsgab->tsab", selector, arrived, precision=lax.Precision.HIGHEST)
        * live_wide
    )
    return (site_density, totals.astype(jnp.bfloat16))


def solution(mesh):
    in_specs = (
        P(("grp", "mat"), None, None),
        P(("grp", "mat"), None),
        P("mat", None, None, None),
        P("mat", None),
        P(("grp", "mat"), None),
        P(("grp", "mat")),
    )
    out_specs = (P(("grp", "mat"), None), P("mat", None, "grp", None))
    return jax.shard_map(
        per_device, mesh=mesh, in_specs=in_specs, out_specs=out_specs, check_vma=False
    )
```

profile of v0, /device:TPU:0, one launch (start us, length us, event | category | flops | bytes accessed | tf_op | source)
XLA Modules:
  0.0 356.7 jit_solution(6114174690834686874)
XLA Ops:
  4.6 13.1 %all-reduce = s32[8]{0:T(128)S(1)} all-reduce(s32[8]{0:T(128)S(1)} %dynamic-update-slice), channel_id=1, replica_groups=mesh['grp'=4,'mat'=8] {'mat'}, use_global_device_ids=true, to_apply=%add | all-reduce | flops 8 | bytes 64
  23.4 3.6 %all-to-all-start = ((bf16[8,5,128,128]{3,2,1,0:T(8,128)(2,1)}), bf16[8,5,128,128]{3,2,1,0:T(8,128)(2,1)S(1)}, u32[]{:S(2)}, u32[]{:S(2)}) async-start(bf16[8,5,128,128]{3,2,1,0:T(8,128)(2,1)} %select_multiply_fusion), calls=%async_computation | async-start | bytes 2621440 | tf_op jit(solution)/shard_map/all_to_all | solution.py:26
  29.9 26.0 %all-to-all-done = bf16[8,5,128,128]{3,2,1,0:T(8,128)(2,1)S(1)} async-done(((bf16[8,5,128,128]{3,2,1,0:T(8,128)(2,1)}), bf16[8,5,128,128]{3,2,1,0:T(8,128)(2,1)S(1)}, u32[]{:S(2)}, u32[]{:S(2)}) %all-to-all-start) | async-done | bytes 1310752 | tf_op jit(solution)/shard_map/all_to_all | solution.py:26
  59.8 167.2 %while.14 = (s32[]{:T(128)}, f32[8,5,128,128]{3,2,1,0:T(8,128)}, f32[4,4,256]{2,1,0:T(4,128)S(1)}, s32[4,4,4]{2,1,0:T(4,128)S(1)}, s32[]{:T(128)}, /*index=5*/s3...) while((s32[]{:T(128)}, f32[8,5,128,128]{3,2,1,0:T(8,128)}, ...), condition=%wide.region_4.5_spmd.clone.clone, body=%wide.region_1.4_spmd.clone.clone.sunk | while | flops 1082136832 | bytes 104901624 | solution.py:71
  65.6 5.0 %bitcast_select_fusion.9 = bf16[4,4,128,4,128]{4,3,2,1,0:T(4,128)(2,1)} fusion(bf16[4,4,4,128,128]{3,2,4,1,0:T(4,128)(2,1)} %copy.56, bf16[4,4,4,128,128]{4,3,2,1,0:T(8,128)(2,1)S(1)} %bitcast.80, pred[4,4]{1,0:T(4,128)(4,1)S(1)} %iota_compare_fusion.5), kind=kLoop, calls=%fused_computation.13.clone.1 | loop fusion | flops 1048576 | bytes 6291472 | tf_op jit(solution)/shard_map/while/body/eval_jaxpr/jit(_where)/select_n | solution.py:51
  79.1 5.2 %reshape.366 = f32[4,4,128,4,128]{4,3,2,1,0:T(4,128)} reshape(f32[4,512,512]{2,1,0:T(8,128)} %fusion.56) | data formatting | bytes 8388608 | tf_op jit(solution)/shard_map/while/body/eval_jaxpr/reshape | solution.py:62
  84.3 3.3 select_bitcast_fusion.2
  90.2 9.8 %scatter_fusion = f32[8,5,128,128]{3,2,1,0:T(8,128)S(1)} fusion(f32[8,5,128,128]{3,2,1,0:T(8,128)S(1)} %copy-done, s32[64]{0:T(128)S(1)} %reshape.363, f32[64,128,128]{2,1,0:T(8,128)} %bitcast.81), kind=kCustom, calls=%fused_computation.5.clone.clone.1 | custom fusion | flops 1048576 | bytes 12583424 | tf_op jit(solution)/shard_map/while/body/eval_jaxpr/scatter-add | solution.py:68
  107.4 5.0 %bitcast_select_fusion.9 = bf16[4,4,128,4,128]{4,3,2,1,0:T(4,128)(2,1)} fusion(bf16[4,4,4,128,128]{3,2,4,1,0:T(4,128)(2,1)} %copy.56, bf16[4,4,4,128,128]{4,3,2,1,0:T(8,128)(2,1)S(1)} %bitcast.80, pred[4,4]{1,0:T(4,128)(4,1)S(1)} %iota_compare_fusion.5), kind=kLoop, calls=%fused_computation.13.clone.1 | loop fusion | flops 1048576 | bytes 6291472 | tf_op jit(solution)/shard_map/while/body/eval_jaxpr/jit(_where)/select_n | solution.py:51
  120.9 5.2 %reshape.366 = f32[4,4,128,4,128]{4,3,2,1,0:T(4,128)} reshape(f32[4,512,512]{2,1,0:T(8,128)} %fusion.56) | data formatting | bytes 8388608 | tf_op jit(solution)/shard_map/while/body/eval_jaxpr/reshape | solution.py:62
  126.1 3.3 select_bitcast_fusion.2
  132.0 9.8 %scatter_fusion = f32[8,5,128,128]{3,2,1,0:T(8,128)S(1)} fusion(f32[8,5,128,128]{3,2,1,0:T(8,128)S(1)} %copy-done, s32[64]{0:T(128)S(1)} %reshape.363, f32[64,128,128]{2,1,0:T(8,128)} %bitcast.81), kind=kCustom, calls=%fused_computation.5.clone.clone.1 | custom fusion | flops 1048576 | bytes 12583424 | tf_op jit(solution)/shard_map/while/body/eval_jaxpr/scatter-add | solution.py:68
  149.2 5.0 %bitcast_select_fusion.9 = bf16[4,4,128,4,128]{4,3,2,1,0:T(4,128)(2,1)} fusion(bf16[4,4,4,128,128]{3,2,4,1,0:T(4,128)(2,1)} %copy.56, bf16[4,4,4,128,128]{4,3,2,1,0:T(8,128)(2,1)S(1)} %bitcast.80, pred[4,4]{1,0:T(4,128)(4,1)S(1)} %iota_compare_fusion.5), kind=kLoop, calls=%fused_computation.13.clone.1 | loop fusion | flops 1048576 | bytes 6291472 | tf_op jit(solution)/shard_map/while/body/eval_jaxpr/jit(_where)/select_n | solution.py:51
  162.7 5.2 %reshape.366 = f32[4,4,128,4,128]{4,3,2,1,0:T(4,128)} reshape(f32[4,512,512]{2,1,0:T(8,128)} %fusion.56) | data formatting | bytes 8388608 | tf_op jit(solution)/shard_map/while/body/eval_jaxpr/reshape | solution.py:62
  167.9 3.3 select_bitcast_fusion.2
  173.8 9.8 %scatter_fusion = f32[8,5,128,128]{3,2,1,0:T(8,128)S(1)} fusion(f32[8,5,128,128]{3,2,1,0:T(8,128)S(1)} %copy-done, s32[64]{0:T(128)S(1)} %reshape.363, f32[64,128,128]{2,1,0:T(8,128)} %bitcast.81), kind=kCustom, calls=%fused_computation.5.clone.clone.1 | custom fusion | flops 1048576 | bytes 12583424 | tf_op jit(solution)/shard_map/while/body/eval_jaxpr/scatter-add | solution.py:68
  191.0 5.0 %bitcast_select_fusion.9 = bf16[4,4,128,4,128]{4,3,2,1,0:T(4,128)(2,1)} fusion(bf16[4,4,4,128,128]{3,2,4,1,0:T(4,128)(2,1)} %copy.56, bf16[4,4,4,128,128]{4,3,2,1,0:T(8,128)(2,1)S(1)} %bitcast.80, pred[4,4]{1,0:T(4,128)(4,1)S(1)} %iota_compare_fusion.5), kind=kLoop, calls=%fused_computation.13.clone.1 | loop fusion | flops 1048576 | bytes 6291472 | tf_op jit(solution)/shard_map/while/body/eval_jaxpr/jit(_where)/select_n | solution.py:51
  204.5 5.2 %reshape.366 = f32[4,4,128,4,128]{4,3,2,1,0:T(4,128)} reshape(f32[4,512,512]{2,1,0:T(8,128)} %fusion.56) | data formatting | bytes 8388608 | tf_op jit(solution)/shard_map/while/body/eval_jaxpr/reshape | solution.py:62
  209.7 3.3 select_bitcast_fusion.2
  215.6 9.8 %scatter_fusion = f32[8,5,128,128]{3,2,1,0:T(8,128)S(1)} fusion(f32[8,5,128,128]{3,2,1,0:T(8,128)S(1)} %copy-done, s32[64]{0:T(128)S(1)} %reshape.363, f32[64,128,128]{2,1,0:T(8,128)} %bitcast.81), kind=kCustom, calls=%fused_computation.5.clone.clone.1 | custom fusion | flops 1048576 | bytes 12583424 | tf_op jit(solution)/shard_map/while/body/eval_jaxpr/scatter-add | solution.py:68
  232.0 33.9 %all_to_all.15 = f32[8,5,4,32,128]{4,0,3,1,2:T(8,128)S(1)} all-to-all(f32[8,5,4,32,128]{4,0,3,1,2:T(8,128)S(1)} %copy.39), channel_id=1, replica_groups=mesh['grp'=4,'mat'=8] {'grp'}, dimensions={2} | all-to-all | bytes 5242880 | tf_op jit(solution)/shard_map/all_to_all | solution.py:85
  265.9 3.2 copy.40
  269.1 3.6 %all-to-all-start.2 = ((f32[8,5,4,32,128]{4,2,3,1,0:T(4,128)}), f32[8,5,4,32,128]{4,2,3,1,0:T(4,128)S(1)}, u32[]{:S(2)}, u32[]{:S(2)}) async-start(f32[8,5,4,32,128]{4,2,3,1,0:T(4,128)} %copy.40), calls=%async_computation.2 | async-start | bytes 5242880 | tf_op jit(solution)/shard_map/all_to_all | solution.py:84
  273.5 78.7 %all-reduce.1 = s32[32]{0:T(128)S(1)} all-reduce(s32[32]{0:T(128)S(1)} %dynamic-update-slice.1), channel_id=1, replica_groups=mesh['grp'=4,'mat'=8] {'grp','mat'}, use_global_device_ids=true, to_apply=%add.1 | all-reduce | flops 32 | bytes 256
  (126 shorter events, 100.2 us)
Async XLA Ops:
  22.2 4.8 %copy-start.4 = (s32[16,4]{0,1:T(4,128)S(1)}, s32[16,4]{0,1:T(4,128)}, u32[]{:S(2)}) copy-start(s32[16,4]{0,1:T(4,128)} %param.12) | copy-start | bytes 772
  22.2 4.9 %copy-start.5 = (s32[16]{0:T(128)S(1)}, s32[16]{0:T(128)}, u32[]{:S(2)}) copy-start(s32[16]{0:T(128)} %param.13) | copy-start | bytes 196
  22.2 5.0 %copy-start.3 = (f32[16,256]{1,0:T(8,128)S(1)}, f32[16,256]{1,0:T(8,128)}, u32[]{:S(2)}) copy-start(f32[16,256]{1,0:T(8,128)} %param.9) | copy-start | bytes 49156
  23.4 32.5 %all-to-all-start = ((bf16[8,5,128,128]{3,2,1,0:T(8,128)(2,1)}), bf16[8,5,128,128]{3,2,1,0:T(8,128)(2,1)S(1)}, u32[]{:S(2)}, u32[]{:S(2)}) async-start(bf16[8,5,128,128]{3,2,1,0:T(8,128)(2,1)} %select_multiply_fusion), calls=%async_computation | async-start | bytes 2621440 | tf_op jit(solution)/shard_map/all_to_all | solution.py:26
  73.4 2.8 copy-start.2
  87.6 2.5 copy-start
  100.0 1.6 copy-start.1
  115.2 2.8 copy-start.2
  129.4 2.5 copy-start
  141.8 1.6 copy-start.1
  157.0 2.8 copy-start.2
  171.2 2.5 copy-start
  183.6 1.6 copy-start.1
  198.8 2.8 copy-start.2
  213.0 2.5 copy-start
  225.4 1.6 copy-start.1
  269.1 83.8 %all-to-all-start.2 = ((f32[8,5,4,32,128]{4,2,3,1,0:T(4,128)}), f32[8,5,4,32,128]{4,2,3,1,0:T(4,128)S(1)}, u32[]{:S(2)}, u32[]{:S(2)}) async-start(f32[8,5,4,32,128]{4,2,3,1,0:T(4,128)} %copy.40), calls=%async_computation.2 | async-start | bytes 5242880 | tf_op jit(solution)/shard_map/all_to_all | solution.py:84
where the time goes:
time: 359 us; the launch traced here: 357 us
  blocking collectives  126 us (35%)
  local copies, waits for them, and re-layouts  89.2 us (25%)
  other arithmetic  83.4 us (23%)
  waiting for transfers between devices  26 us (7%)
  matrix products  24.1 us (7%)
  starting transfers between devices  7.19 us (2%)
    unnamed x2, blocking collectives  91.8 us
    scatter-add x4, other arithmetic, integrate(): ham_region = ham_region.at[row_index, offset].add(increment)  39.4 us
    all_to_all x1, blocking collectives, per_device(): lax.all_to_all(pieces, 'grp', split_axis=2, concat_axis=2, tiled=True)  33.9 us
    all_to_all x1, waiting for transfers between devices, per_device(): lax.all_to_all(outgoing, 'mat', split_axis=0, concat_axis=0, tiled=True)  26 us
    reshape x4, local copies, waits for them, and re-layouts, integrate(): ham_batch.reshape(4, slot_count, block_size, slot_count, block_size)  20.9 us
    select_n x4, other arithmetic, integrate(): jnp.where(upper_half[None, :, :, None, None], gathered_tiles, jnp.swapaxe...  19.9 us
    gather x8, local copies, waits for them, and re-layouts, integrate(): gathered_tiles = region[row_index, offset]  19.3 us
    select_n x4, other arithmetic, integrate(): jnp.where(upper_half[None, :, :, None, None], ham_tiles, jnp.zeros_like(h...  13.1 us
  transfers between devices with their start and end apart: 2, of which 1 were waited for; matrix products, arithmetic and copies ran while one was open for 1% of the time, Pallas kernels for 0%

commit v1 on v0

v1 whole, which is shorter than its diff:
```python
import functools

import jax
import jax.numpy as jnp
from jax import lax
from jax.experimental import pallas as pl
from jax.experimental.pallas import tpu as pltpu
from jax.sharding import PartitionSpec as P

MIB = 1 << 20


def pick_kernel(rows, live, density, out, sems):
    count, span = out.shape[0], out.shape[1]

    def copy(d):
        return pltpu.make_async_copy(density.at[rows[d]], out.at[d], sems.at[d])

    for d in range(count):
        copy(d).start()

    def scale(d, carry):
        copy(d).wait()
        for o in range(span):
            factor = (live[rows[d], o] * (1 if o == 0 else 2)).astype(jnp.float32)
            out[d, o] = (out[d, o].astype(jnp.float32) * factor).astype(jnp.bfloat16)
        return carry

    lax.fori_loop(0, count, scale, 0)


def pick_rows(rows, live, density):
    count = rows.shape[0]
    return pl.pallas_call(
        pick_kernel,
        out_shape=jax.ShapeDtypeStruct((count,) + density.shape[1:], jnp.bfloat16),
        in_specs=[
            pl.BlockSpec(memory_space=pltpu.SMEM),
            pl.BlockSpec(memory_space=pltpu.SMEM),
            pl.BlockSpec(memory_space=pl.ANY),
        ],
        out_specs=pl.BlockSpec(memory_space=pltpu.VMEM),
        scratch_shapes=[pltpu.SemaphoreType.DMA((count,))],
        compiler_params=pltpu.CompilerParams(vmem_limit_bytes=16 * MIB),
        name="pick",
    )(rows, live, density)


def turn_kernel(live, values, out):
    batch = pl.program_id(0)
    turned = values[0].astype(jnp.float32).T
    index = lax.broadcasted_iota(jnp.int32, turned.shape, 0)
    out[0] = jnp.where(index < live[batch], turned, 0.0).astype(jnp.bfloat16)


def turn_values(live, values):
    batches, points, width = values.shape
    return pl.pallas_call(
        turn_kernel,
        out_shape=jax.ShapeDtypeStruct((batches, width, points), jnp.bfloat16),
        grid_spec=pltpu.PrefetchScalarGridSpec(
            num_scalar_prefetch=1,
            grid=(batches,),
            in_specs=[pl.BlockSpec((1, points, width), lambda b, live: (b, 0, 0))],
            out_specs=pl.BlockSpec((1, width, points), lambda b, live: (b, 0, 0)),
        ),
        compiler_params=pltpu.CompilerParams(vmem_limit_bytes=16 * MIB),
        cost_estimate=pl.CostEstimate(
            flops=20_000_000_000, bytes_accessed=4 * batches * points * width, transcendentals=0
        ),
        name="turn",
    )(live, values)


def integrate_kernel(groups, blocks, turned, weights, region, site_out, pieces, matrix, total):
    holders, span, block, _ = region.shape
    batches, width, points = turned.shape
    slots = width // block
    half = width // 2
    matrix[...] = jnp.zeros_like(matrix)
    total[...] = jnp.zeros_like(total)

    def one(b, carry):
        ids = [blocks[b, k] for k in range(slots)]
        homes = [lax.rem(i, holders) for i in ids]
        pairs = [(k, l) for k in range(slots) for l in range(k, slots)]
        for k, l in pairs:
            matrix[k * block : (k + 1) * block, l * block : (l + 1) * block] = region[
                homes[k], ids[l] - ids[k]
            ]
        values = turned[b]
        lower = values[half:]
        product_top = jnp.dot(matrix[:half, :], values, preferred_element_type=jnp.float32)
        product_low = jnp.dot(matrix[half:, half:], lower, preferred_element_type=jnp.float32)
        wide = values.astype(jnp.float32)
        site = jnp.sum(product_top * wide[:half] + product_low * wide[half:], axis=0, keepdims=True)
        site_out[pl.ds(b, 1), :] = site
        potential = weights[pl.ds(b, 1), :] * site / jnp.sqrt(1.0 + site * site)
        weighted = (potential * wide).astype(jnp.bfloat16)
        rows = (((1,), (1,)), ((), ()))
        ham_top = lax.dot_general(values[:half], weighted, rows, preferred_element_type=jnp.float32)
        ham_low = lax.dot_general(lower, weighted[half:], rows, preferred_element_type=jnp.float32)
        for k, l in pairs:
            low = k * block >= half
            source, column = (ham_low, l * block - half) if low else (ham_top, l * block)
            row = k * block - half if low else k * block
            total[homes[k], ids[l] - ids[k]] += source[row : row + block, column : column + block]
        return carry

    lax.fori_loop(0, batches, one, 0)
    part = block // groups

    def store(h, carry):
        for g in range(groups):
            for o in range(span):
                pieces[g * holders + h, o] = total[h, o, g * part : (g + 1) * part, :].astype(
                    jnp.bfloat16
                )
        return carry

    lax.fori_loop(0, holders, store, 0)


def integrate(groups, blocks, turned, weights, region):
    batches, width, points = turned.shape
    holders, span, block, _ = region.shape
    vmem = pl.BlockSpec(memory_space=pltpu.VMEM)
    return pl.pallas_call(
        functools.partial(integrate_kernel, groups),
        out_shape=(
            jax.ShapeDtypeStruct((batches, points), jnp.float32),
            jax.ShapeDtypeStruct((groups * holders, span, block // groups, block), jnp.bfloat16),
        ),
        in_specs=[pl.BlockSpec(memory_space=pltpu.SMEM), vmem, vmem, vmem],
        out_specs=(vmem, vmem),
        scratch_shapes=[
            pltpu.VMEM((width, width), jnp.bfloat16),
            pltpu.VMEM((holders, span, block, block), jnp.float32),
        ],
        compiler_params=pltpu.CompilerParams(vmem_limit_bytes=40 * MIB),
        name="integrate",
    )(blocks, turned, weights, region)


def finish_kernel(rows, live, arrived, out, total):
    sources, span = arrived.shape[0], arrived.shape[1]
    local = out.shape[0]
    total[...] = jnp.zeros_like(total)

    def add(s, carry):
        total[rows[s]] += arrived[s].astype(jnp.float32)
        return carry

    lax.fori_loop(0, sources, add, 0)

    def store(t, carry):
        for o in range(span):
            out[t, o] = (total[t, o] * live[t, o].astype(jnp.float32)).astype(jnp.bfloat16)
        return carry

    lax.fori_loop(0, local, store, 0)


def finish(rows, live, arrived):
    local = live.shape[0]
    shape = (local,) + arrived.shape[1:]
    smem = pl.BlockSpec(memory_space=pltpu.SMEM)
    vmem = pl.BlockSpec(memory_space=pltpu.VMEM)
    return pl.pallas_call(
        finish_kernel,
        out_shape=jax.ShapeDtypeStruct(shape, jnp.bfloat16),
        in_specs=[smem, smem, vmem],
        out_specs=vmem,
        scratch_shapes=[pltpu.VMEM(shape, jnp.float32)],
        compiler_params=pltpu.CompilerParams(vmem_limit_bytes=24 * MIB),
        name="finish",
    )(rows, live, arrived)


def per_device(basis_values, weights, density, block_live, batch_blocks, live_functions):
    holders = lax.axis_size("mat")
    groups = lax.axis_size("grp")
    holder = lax.axis_index("mat")
    first = jnp.min(batch_blocks)
    firsts = lax.psum(jnp.where(jnp.arange(holders) == holder, first, 0), "mat")
    wanted = (firsts + (holder - firsts) % holders - holder) // holders
    outgoing = pick_rows(wanted, block_live, density)
    region = lax.all_to_all(outgoing, "mat", split_axis=0, concat_axis=0, tiled=True)
    turned = turn_values(live_functions, basis_values)
    all_rows = lax.all_gather(wanted, "grp", axis=0, tiled=True)
    site_density, pieces = integrate(groups, batch_blocks, turned, weights, region)
    arrived = lax.all_to_all(pieces, ("grp", "mat"), split_axis=0, concat_axis=0, tiled=True)
    hamiltonian = finish(all_rows, block_live, arrived)
    return site_density, hamiltonian


def solution(mesh):
    in_specs = (
        P(("grp", "mat"), None, None),
        P(("grp", "mat"), None),
        P("mat", None, None, None),
        P("mat", None),
        P(("grp", "mat"), None),
        P(("grp", "mat")),
    )
    out_specs = (P(("grp", "mat"), None), P("mat", None, "grp", None))
    return jax.shard_map(
        per_device, mesh=mesh, in_specs=in_specs, out_specs=out_specs, check_vma=False
    )
```

time: 359 us -> 112 us (0.31)
  blocking collectives: 126 us -> 22.2 us
  other arithmetic: 83.4 us -> 2.09 us
  local copies, waits for them, and re-layouts: 89.2 us -> 10.5 us
  matrix products: 24.1 us -> 0 us
  Pallas kernels: 0 us -> 22.2 us
  waiting for transfers between devices: 26 us -> 45.7 us
    unnamed x2 -> x1, blocking collectives: 91.8 us -> 9.06 us
    scatter-add x4 -> x0, other arithmetic: 39.4 us -> none  [integrate(): ham_region = ham_region.at[row_index, offset].add(increment)]
    select_n x14 -> x1, other arithmetic: 36.1 us -> 0.65 us  [per_device(): firsts = lax.psum(jnp.where(jnp.arange(holders) == holder, first, 0), 'mat')]
    all_to_all x1 -> x0, blocking collectives: 33.9 us -> none  [per_device(): lax.all_to_all(pieces, 'grp', split_axis=2, concat_axis=2, tiled=True)]
    reshape x12 -> x0, local copies, waits for them, and re-layouts: 32.7 us -> none  [the longest x4 20.9 us: integrate(): ham_batch.reshape(4, slot_count, block_size, slot_count, block_size)]
    gather x12 -> x0, local copies, waits for them, and re-layouts: 26.1 us -> none  [the longest x8 19.3 us: integrate(): gathered_tiles = region[row_index, offset]]
    dot_general x9 -> x0, matrix products: 24.1 us -> none  [the longest x4 11.5 us: integrate(): jnp.einsum('brf,brg->bfg', values, weighted, preferred_element_type=jnp.f...]
    all_to_all x1, waiting for transfers between devices: 0.01 us -> 24 us  [per_device(): lax.all_to_all(pieces, ('grp', 'mat'), split_axis=0, concat_axis=0, tiled...]
  transfers between devices with their start and end apart: 2 -> 2, of which waited for: 1 -> 2; matrix products, arithmetic and copies ran while one was open for 1% -> 0% of each run, Pallas kernels for 0% -> 3%
where the time goes in v1:
time: 112 us; the launch traced here: 111 us
  waiting for transfers between devices  45.7 us (41%)
  blocking collectives  22.2 us (20%)
  Pallas kernels  22.2 us (20%)
  local copies, waits for them, and re-layouts  10.5 us (9%)
  starting transfers between devices  7.06 us (6%)
  other arithmetic  2.09 us (2%)
  between operations  1.38 us (1%)
    all_to_all x1, waiting for transfers between devices, per_device(): lax.all_to_all(pieces, ('grp', 'mat'), split_axis=0, concat_axis=0, tiled...  24 us
    all_to_all x1, waiting for transfers between devices, per_device(): lax.all_to_all(outgoing, 'mat', split_axis=0, concat_axis=0, tiled=True)  21.7 us
    psum x1, blocking collectives, per_device(): firsts = lax.psum(jnp.where(jnp.arange(holders) == holder, first, 0), 'mat')  13.1 us
    pallas_call x1, Pallas kernels, integrate(): pl.pallas_call(functools.partial(integrate_kernel, groups), out_shape=(ja...  12.9 us
    unnamed x18, local copies, waits for them, and re-layouts  10.5 us
    unnamed x1, blocking collectives  9.06 us
    pallas_call x1, Pallas kernels, pick_rows(): pl.pallas_call(pick_kernel, out_shape=jax.ShapeDtypeStruct((count,) + den...  3.86 us
    all_to_all x1, starting transfers between devices, per_device(): lax.all_to_all(outgoing, 'mat', split_axis=0, concat_axis=0, tiled=True)  3.58 us
  transfers between devices with their start and end apart: 2, of which 2 were waited for; matrix products, arithmetic and copies ran while one was open for 0% of the time, Pallas kernels for 3%

profile of v1, /device:TPU:0, one launch (start us, length us, event | category | flops | bytes accessed | tf_op | source)
XLA Modules:
  0.0 111.1 jit_solution(1207272232086924014)
XLA Ops:
  0.6 1.3 %reduce_min.9 = s32[]{:T(128)} reduce(s32[16,4]{0,1:T(4,128)} %param.10, s32[]{:T(128)} %constant.28.clone.1), dimensions={0,1}, to_apply=%region_0.0 | reduce | flops 63 | bytes 264 | tf_op jit(solution)/shard_map/reduce_min | solution.py:184
  2.0 0.6 compare_select_fusion.2
  2.6 13.1 %psum.7 = s32[8]{0:T(128)S(1)} all-reduce(s32[8]{0:T(128)S(1)} %compare_select_fusion.2), channel_id=1, replica_groups=mesh['grp'=4,'mat'=8] {'mat'}, use_global_device_ids=true, to_apply=%region_1.2 | all-reduce | flops 8 | bytes 64 | tf_op jit(solution)/shard_map/psum | solution.py:185
  15.7 0.8 copy.8.live
  16.5 1.2 %dynamic-slice = u32[1]{0:T(128)} dynamic-slice(u32[32]{0:T(128)} %constant.41, u32[]{:T(128)S(6)} %add.14), dynamic_slice_sizes={1} | dynamic-slice | bytes 12
  18.4 0.1 fusion.2
  18.5 2.1 %copy-done.2 = bf16[24,5,128,128]{3,2,1,0:T(8,128)(2,1)S(1)} copy-done((bf16[24,5,128,128]{3,2,1,0:T(8,128)(2,1)S(1)}, bf16[24,5,128,128]{3,2,1,0:T(8,128)(2,1)}, u32[]{:S(2)}) %copy-start.2) | copy-done | bytes 3932184
  20.6 3.9 %pick.1 = bf16[8,5,128,128]{3,2,1,0:T(8,128)(2,1)} custom-call(s32[8]{0:T(128)S(1)} %get-tuple-element.7.rows, s32[24,5]{1,0:T(8,128)S(1)} %copy.8.live, bf16[24,5,128,128]{3,2,1,0:T(8,128)(2,1)S(1)} %copy-done.2), custom_call_target="tpu_custom_call" | custom-call | tf_op jit(solution)/shard_map/pick/pallas_call | solution.py:34
  24.5 0.0 copy-start.6
  24.5 0.0 copy-start.5
  24.5 3.6 %all-to-all-start = ((bf16[8,5,128,128]{3,2,1,0:T(8,128)(2,1)}), bf16[8,5,128,128]{3,2,1,0:T(8,128)(2,1)S(1)}, u32[]{:S(2)}, u32[]{:S(2)}) async-start(bf16[8,5,128,128]{3,2,1,0:T(8,128)(2,1)} %pick.1), calls=%async_computation | async-start | bytes 2621440 | tf_op jit(solution)/shard_map/all_to_all | solution.py:188
  28.1 0.0 copy-done.6
  28.1 0.1 copy.9.blocks
  28.2 0.0 copy-done.5
  28.2 2.2 %copy-done.4 = bf16[16,256,512]{2,1,0:T(8,128)(2,1)S(1)} copy-done((bf16[16,256,512]{2,1,0:T(8,128)(2,1)S(1)}, bf16[16,256,512]{2,1,0:T(8,128)(2,1)}, u32[]{:S(2)}) %copy-start.4) | copy-done | bytes 4194328
  30.4 3.0 %turn.1.turned = bf16[16,512,256]{2,1,0:T(8,128)(2,1)S(1)} custom-call(s32[16]{0:T(128)S(1)} %copy-done.5, bf16[16,256,512]{2,1,0:T(8,128)(2,1)S(1)} %copy-done.4), custom_call_target="tpu_custom_call" | custom-call | flops 20000000000 | bytes 8388608 | tf_op jit(solution)/shard_map/turn/pallas_call | solution.py:58
  33.4 1.9 %copy-done = bf16[16,512,256]{2,1,0:T(8,128)(2,1)} copy-done((bf16[16,512,256]{2,1,0:T(8,128)(2,1)}, bf16[16,512,256]{2,1,0:T(8,128)(2,1)S(1)}, u32[]{:S(2)}) %copy-start) | copy-done | bytes 4194328
  35.3 21.7 %all-to-all-done.region = bf16[8,5,128,128]{3,2,1,0:T(8,128)(2,1)S(1)} async-done(((bf16[8,5,128,128]{3,2,1,0:T(8,128)(2,1)}), bf16[8,5,128,128]{3,2,1,0:T(8,128)(2,1)S(1)}, u32[]{:S(2)}, u32[]{:S(2)}) %all-to-all-start) | async-done | bytes 1310752 | tf_op jit(solution)/shard_map/all_to_all | solution.py:188
  57.0 2.2 %copy-done.1 = bf16[16,512,256]{2,1,0:T(8,128)(2,1)S(1)} copy-done((bf16[16,512,256]{2,1,0:T(8,128)(2,1)S(1)}, bf16[16,512,256]{2,1,0:T(8,128)(2,1)}, u32[]{:S(2)}) %copy-start.1) | copy-done | bytes 4194328
  59.2 12.9 %integrate.1 = (f32[16,256]{1,0:T(8,128)}, bf16[32,5,32,128]{3,2,1,0:T(8,128)(2,1)}) custom-call(s32[16,4]{1,0:T(8,128)S(1)} %copy.9.blocks, bf16[16,512,256]{2,1,0:T(8,128)(2,1)S(1)} %copy-done.1, f32[16,256]{1,0:T(8,128)S(1)} %copy-done.3, bf16[8,5,128,128]{3,2,1,0:T(8,128)(2,1)S(1)} %all-to-all-done.region), custom_call_target="tpu_custom_call" | custom-call | tf_op jit(solution)/shard_map/integrate/pallas_call | solution.py:128
  72.0 3.5 %all-to-all-start.1 = ((bf16[32,5,32,128]{3,2,1,0:T(8,128)(2,1)}), bf16[32,5,32,128]{3,2,1,0:T(8,128)(2,1)S(1)}, u32[]{:S(2)}, u32[]{:S(2)}) async-start(bf16[32,5,32,128]{3,2,1,0:T(8,128)(2,1)} %get-tuple-element.5), calls=%async_computation.1 | async-start | bytes 2621440 | tf_op jit(solution)/shard_map/all_to_all | solution.py:192
  75.5 9.1 %all-reduce.rows = s32[32]{0:T(128)S(1)} all-reduce(s32[32]{0:T(128)S(1)} %get-tuple-element.6), channel_id=1, replica_groups=mesh['grp'=4,'mat'=8] {'grp'}, use_global_device_ids=true, to_apply=%add | all-reduce | flops 32 | bytes 256
  84.6 24.0 %all-to-all-done.1.arrived = bf16[32,5,32,128]{3,2,1,0:T(8,128)(2,1)S(1)} async-done(((bf16[32,5,32,128]{3,2,1,0:T(8,128)(2,1)}), bf16[32,5,32,128]{3,2,1,0:T(8,128)(2,1)S(1)}, u32[]{:S(2)}, u32[]{:S(2)}) %all-to-all-start.1) | async-done | bytes 1310752 | tf_op jit(solution)/shard_map/all_to_all | solution.py:192
  108.6 2.5 %finish.1 = bf16[24,5,32,128]{3,2,1,0:T(8,128)(2,1)} custom-call(s32[32]{0:T(128)S(1)} %all-reduce.rows, s32[24,5]{1,0:T(8,128)S(1)} %copy.8.live, bf16[32,5,32,128]{3,2,1,0:T(8,128)(2,1)S(1)} %all-to-all-done.1.arrived), custom_call_target="tpu_custom_call" | custom-call | tf_op jit(solution)/shard_map/finish/pallas_call | solution.py:169
  (7 shorter events, 0.0 us)
Async XLA Ops:
  18.5 2.1 %copy-start.2 = (bf16[24,5,128,128]{3,2,1,0:T(8,128)(2,1)S(1)}, bf16[24,5,128,128]{3,2,1,0:T(8,128)(2,1)}, u32[]{:S(2)}) copy-start(bf16[24,5,128,128]{3,2,1,0:T(8,128)(2,1)} %density.1) | copy-start | bytes 11796484
  24.5 3.6 %copy-start.6 = (s32[16,4]{0,1:T(4,128)S(1)}, s32[16,4]{0,1:T(4,128)}, u32[]{:S(2)}) copy-start(s32[16,4]{0,1:T(4,128)} %param.10) | copy-start | bytes 772
  24.5 3.7 %copy-start.5 = (s32[16]{0:T(128)S(1)}, s32[16]{0:T(128)}, u32[]{:S(2)}) copy-start(s32[16]{0:T(128)} %live.3) | copy-start | bytes 196
  24.5 32.5 %all-to-all-start = ((bf16[8,5,128,128]{3,2,1,0:T(8,128)(2,1)}), bf16[8,5,128,128]{3,2,1,0:T(8,128)(2,1)S(1)}, u32[]{:S(2)}, u32[]{:S(2)}) async-start(bf16[8,5,128,128]{3,2,1,0:T(8,128)(2,1)} %pick.1), calls=%async_computation | async-start | bytes 2621440 | tf_op jit(solution)/shard_map/all_to_all | solution.py:188
  28.2 2.2 %copy-start.4 = (bf16[16,256,512]{2,1,0:T(8,128)(2,1)S(1)}, bf16[16,256,512]{2,1,0:T(8,128)(2,1)}, u32[]{:S(2)}) copy-start(bf16[16,256,512]{2,1,0:T(8,128)(2,1)} %values.1) | copy-start | bytes 12582916
  30.4 26.6 %copy-start.3 = (f32[16,256]{1,0:T(8,128)S(1)}, f32[16,256]{1,0:T(8,128)}, u32[]{:S(2)}) copy-start(f32[16,256]{1,0:T(8,128)} %weights.1) | copy-start | bytes 49156
  33.4 1.9 %copy-start = (bf16[16,512,256]{2,1,0:T(8,128)(2,1)}, bf16[16,512,256]{2,1,0:T(8,128)(2,1)S(1)}, u32[]{:S(2)}) copy-start(bf16[16,512,256]{2,1,0:T(8,128)(2,1)S(1)} %turn.1.turned) | copy-start | bytes 12582916
  57.0 2.2 %copy-start.1 = (bf16[16,512,256]{2,1,0:T(8,128)(2,1)S(1)}, bf16[16,512,256]{2,1,0:T(8,128)(2,1)}, u32[]{:S(2)}) copy-start(bf16[16,512,256]{2,1,0:T(8,128)(2,1)} %copy-done) | copy-start | bytes 12582916
  72.0 36.6 %all-to-all-start.1 = ((bf16[32,5,32,128]{3,2,1,0:T(8,128)(2,1)}), bf16[32,5,32,128]{3,2,1,0:T(8,128)(2,1)S(1)}, u32[]{:S(2)}, u32[]{:S(2)}) async-start(bf16[32,5,32,128]{3,2,1,0:T(8,128)(2,1)} %get-tuple-element.5), calls=%async_computation.1 | async-start | bytes 2621440 | tf_op jit(solution)/shard_map/all_to_all | solution.py:192
